TPU v7x, 32 devices: a whole 2x2x4 slice. The times are simulated.
32 devices in a mesh: replica: 2 (over core), fsdp: 16 (over z, y, x).
Axes of the slice: x: 2, y: 2, z: 4, core: 2. Of those that a mesh axis runs over, the one named last changes fastest.
Arguments:
- activations: bfloat16 [16384, 4096], P(('replica', 'fsdp')), may hold values from -6 to 6
- queries: bfloat16 [16384, 2048], P(('replica', 'fsdp')), may hold values from -60 to 60
- out_grad: bfloat16 [16384, 2048], P(('replica', 'fsdp')), may hold values from -6 to 6
- lengths: int32 [64], P(('replica', 'fsdp')), may hold values from 32 to 256
- norm_gain: float32 [4096], replicated, may hold values from 0.5 to 7
- key_master: float32 [4096, 512], P('fsdp'), may hold values from -0.09375 to 0.09375
- value_master: float32 [4096, 512], P('fsdp'), may hold values from -0.09375 to 0.09375
Outputs:
- key_direction: float32 [4096, 512], P('fsdp')
- value_direction: float32 [4096, 512], P('fsdp')
All inputs are finite; a program needn't handle non-finite values.
Results may differ from a plain program's by a relative error of at most 0.009.
The roundings to bfloat16 on the way count: a program that leaves them out, or rounds other values in their place, can miss the bound.
Values may be sent and summed in bfloat16 or wider, within the bound.
A program may use at most 128 MiB of HBM per device.

v0:
```python
import jax
import jax.numpy as jnp
from jax import lax
from jax.sharding import PartitionSpec as P

D = 4096
HD = 128
KVH = 4
GROUP = 4
LEN = 256


def attend(query_seq, key_seq, value_seq, grad_seq, length):
    scale_factor = 1.0 / HD**0.5
    positions = jnp.arange(LEN, dtype=jnp.int32)
    allowed = (positions[None, :] <= positions[:, None]) & (positions[None, :] < length)
    query_float = query_seq.astype(jnp.float32).reshape(LEN, KVH, GROUP, HD)
    key_float = key_seq.astype(jnp.float32).reshape(LEN, KVH, HD)
    value_float = value_seq.astype(jnp.float32).reshape(LEN, KVH, HD)
    scores = jnp.einsum("qhgd,khd->hgqk", query_float, key_float) * scale_factor
    scores = jnp.where(allowed[None, None], scores, jnp.float32(-1e30))
    row_peak = jnp.max(scores, axis=-1, keepdims=True)
    exponent = jnp.exp(scores - row_peak)
    probs = exponent / jnp.sum(exponent, axis=-1, keepdims=True)
    probs_low = lax.optimization_barrier(probs.astype(jnp.bfloat16))
    probs_back = probs_low.astype(jnp.float32)
    attended = jnp.einsum("hgqk,khd->qhgd", probs_back, value_float).astype(jnp.bfloat16)
    attended = lax.optimization_barrier(attended).astype(jnp.float32)
    live_rows = (positions < length).astype(jnp.float32)
    grad_float = (
        grad_seq.astype(jnp.float32).reshape(LEN, KVH, GROUP, HD) * live_rows[:, None, None, None]
    )
    row_delta = jnp.transpose(jnp.sum(grad_float * attended, axis=-1), (1, 2, 0))[..., None]
    value_grad = jnp.einsum("hgqk,qhgd->khd", probs_back, grad_float).astype(jnp.bfloat16)
    prob_grad = jnp.einsum("qhgd,khd->hgqk", grad_float, value_float)
    score_grad = lax.optimization_barrier((probs * (prob_grad - row_delta)).astype(jnp.bfloat16))
    key_grad = (
        jnp.einsum("hgqk,qhgd->khd", score_grad.astype(jnp.float32), query_float) * scale_factor
    ).astype(jnp.bfloat16)
    return (key_grad.reshape(LEN, KVH * HD), value_grad.reshape(LEN, KVH * HD))


def transposed_product(columns, combined):
    return lax.dot_general(
        columns, combined, (((0,), (0,)), ((), ())), preferred_element_type=jnp.float32
    )


def local(activations, queries, out_grad, lengths, norm_gain, key_master, value_master):
    tok_rows = activations.shape[0]
    width = key_master.shape[1]
    shard_rows = key_master.shape[0]
    act_float = activations.astype(jnp.float32)
    inverse = lax.rsqrt(jnp.mean(act_float * act_float, axis=-1, keepdims=True) + 1e-05)
    normed = (act_float * inverse * norm_gain[None, :]).astype(jnp.bfloat16)
    columns = normed
    key_sum = jnp.dot(
        columns,
        lax.all_gather(key_master.astype(jnp.bfloat16), "fsdp", axis=0, tiled=True),
        preferred_element_type=jnp.float32,
    )
    value_sum = jnp.dot(
        columns,
        lax.all_gather(value_master.astype(jnp.bfloat16), "fsdp", axis=0, tiled=True),
        preferred_element_type=jnp.float32,
    )
    key_proj = key_sum.astype(jnp.bfloat16)
    value_proj = value_sum.astype(jnp.bfloat16)
    seq_count = lengths.shape[0]
    qwidth = queries.shape[1]

    def one_seq(packed):
        return attend(packed[0], packed[1], packed[2], packed[3], packed[4])

    key_grad, value_grad = lax.map(
        one_seq,
        (
            queries.reshape(seq_count, LEN, qwidth),
            key_proj.reshape(seq_count, LEN, width),
            value_proj.reshape(seq_count, LEN, width),
            out_grad.reshape(seq_count, LEN, qwidth),
            lengths,
        ),
    )
    combined = jnp.concatenate(
        [key_grad.reshape(tok_rows, width), value_grad.reshape(tok_rows, width)], axis=1
    )
    replicas = lax.axis_size("replica")
    shards = lax.axis_size("fsdp")
    piece_rows = shard_rows // replicas
    permuted = (
        normed.reshape(tok_rows, shards, replicas, piece_rows)
        .transpose(0, 2, 1, 3)
        .reshape(tok_rows, shards * shard_rows)
    )
    columns = permuted
    owned_grad = lax.psum_scatter(
        transposed_product(columns, combined), ("replica", "fsdp"), scatter_dimension=0, tiled=True
    )
    total_sq = lax.psum(jnp.sum(owned_grad * owned_grad), ("replica", "fsdp"))
    summed = lax.all_gather(owned_grad.astype(jnp.bfloat16), "replica", axis=0, tiled=True).astype(
        owned_grad.dtype
    )
    unit_scale = jnp.sqrt(jnp.float32(2 * D * width)) / jnp.sqrt(total_sq + 1e-06)
    return (unit_scale * summed[:, :width], unit_scale * summed[:, width:])


def solution(mesh):
    in_specs = (
        P(("replica", "fsdp"), None),
        P(("replica", "fsdp"), None),
        P(("replica", "fsdp"), None),
        P(("replica", "fsdp")),
        P(),
        P("fsdp", None),
        P("fsdp", None),
    )
    out_specs = (P("fsdp", None), P("fsdp", None))
    return jax.shard_map(local, mesh=mesh, in_specs=in_specs, out_specs=out_specs, check_vma=False)
```

profile of v0, /device:TPU:7, one launch (start us, length us, event | category | flops | bytes accessed | tf_op | source)
XLA Modules:
  0.0 638.2 jit_solution(8576653580051986996)
XLA Ops:
  7.2 1.8 convert_element_type.74
  9.1 1.8 convert_element_type.72
  11.0 6.5 %copy.41 = bf16[512,4096]{0,1:T(8,128)(2,1)} copy(bf16[512,4096]{1,0:T(8,128)(2,1)} %param.9) | data formatting | bytes 8388608 | tf_op args[0]
  17.4 3.3 fusion.24
  22.1 1.9 copy-done.2
  24.0 2.4 copy.42
  26.4 58.6 %all-gather.5.cloned.1.call-done = bf16[4096,512]{1,0:T(8,128)(2,1)} async-done(((bf16[256,512]{1,0:T(8,128)(2,1)}), bf16[4096,512]{1,0:T(8,128)(2,1)}) %all-gather.5.cloned.1.call-update) | async-done | bytes 4194320 | tf_op jit(solution)/shard_map/all_gather | solution.py:64
  85.0 5.8 convolution_convert_fusion.1
  90.8 71.2 %all-gather.3.cloned.1.call-done = bf16[4096,512]{1,0:T(8,128)(2,1)} async-done(((bf16[256,512]{1,0:T(8,128)(2,1)}), bf16[4096,512]{1,0:T(8,128)(2,1)}) %all-gather.3.cloned.1.call-update) | async-done | bytes 4194320 | tf_op jit(solution)/shard_map/all_gather | solution.py:59
  162.0 6.6 %convolution_convert_fusion.2 = bf16[512,512]{1,0:T(8,128)(2,1)} fusion(bf16[512,4096]{0,1:T(8,128)(2,1)} %copy-done.2, bf16[4096,512]{1,0:T(8,128)(2,1)} %all-gather.3.cloned.1.call-done), kind=kOutput, calls=%fused_computation.44 | convolution fusion | flops 2147745792 | bytes 8912896 | tf_op jit(solution)/shard_map/dot_general | solution.py:57
  168.6 41.5 %while.12 = (s32[]{:T(128)}, bf16[2,256,512]{2,1,0:T(8,128)(2,1)}, bf16[2,256,512]{2,1,0:T(8,128)(2,1)}, bf16[2,256,2048]{2,1,0:T(8,128)(2,1)}, s32[2]{0:T(128)S...) while((s32[]{:T(128)}, bf16[2,256,512]{2,1,0:T(8,128)(2,1)}, ...), condition=%wide.region_5.6_spmd, body=%wide.region_1.5_spmd.sunk | while | flops 1358427136 | bytes 69686040 | solution.py:75
  172.9 1.3 constant_dynamic-slice_fusion.10
  174.7 1.3 constant_dynamic-slice_fusion.9
  176.5 4.4 fusion.74
  181.0 2.6 fusion.75
  193.7 1.3 constant_dynamic-slice_fusion.10
  195.5 1.3 constant_dynamic-slice_fusion.9
  197.3 4.4 fusion.74
  201.7 2.6 fusion.75
  210.1 12.7 %fusion.27 = f32[4096,1024]{1,0:T(8,128)} fusion(bf16[512,4096]{0,1:T(8,128)(2,1)} %bitcast.135, bf16[512,512]{1,0:T(8,128)(2,1)} %bitcast.138, bf16[512,512]{1,0:T(8,128)(2,1)} %bitcast.139), kind=kOutput, calls=%fused_computation.45 | convolution fusion | flops 4297064448 | bytes 22020096 | tf_op jit(solution)/shard_map/dot_general | solution.py:44
  222.9 355.9 %reduce-scatter.2.cloned.1.call-done = f32[128,1024]{1,0:T(8,128)} async-done(((f32[4096,1024]{1,0:T(8,128)}), f32[128,1024]{1,0:T(8,128)}) %reduce-scatter.2.cloned.1.call-update) | async-done | bytes 524304 | tf_op jit(solution)/shard_map/reduce_scatter | solution.py:97
  578.8 2.0 multiply_reduce_fusion
  580.7 44.4 %psum.7 = f32[]{:T(128)} all-reduce(f32[]{:T(128)} %get-tuple-element.93), channel_id=1, replica_groups=mesh['replica'=2,'fsdp'=16] {'replica','fsdp'}, use_global_device_ids=true, to_apply=%region_8.9 | all-reduce | flops 1 | bytes 8 | tf_op jit(solution)/shard_map/psum | solution.py:100
  625.8 4.7 all_gather.11
  (75 shorter events, 24.7 us)
Async XLA Ops:
  7.2 77.8 %all-gather.5.cloned.1.call-start = ((), (), s32[]{:S(2)}) async-start(), calls=%async_computation.2 | async-start | bytes 4456448 | tf_op jit(solution)/shard_map/all_gather | solution.py:64
  9.0 153.0 %all-gather.3.cloned.1.call-start = ((), (), s32[]{:S(2)}) async-start(), calls=%async_computation.1 | async-start | bytes 4456448 | tf_op jit(solution)/shard_map/all_gather | solution.py:59
  10.9 567.9 %reduce-scatter.2.cloned.1.call-start = ((), (), s32[]{:S(2)}) async-start(), calls=%async_computation.3 | async-start | bytes 17301504 | tf_op jit(solution)/shard_map/reduce_scatter | solution.py:97
  10.9 9.8 %copy-start.5 = (f32[4096]{0:T(1024)S(1)}, f32[4096]{0:T(1024)}, u32[]{:S(2)}) copy-start(f32[4096]{0:T(1024)} %param.13) | copy-start | bytes 49156
  17.4 3.5 copy-start.1
  22.1 2.0 copy-start.2
  90.8 77.8 %copy-start.8 = (s32[2]{0:T(128)S(1)}, s32[2]{0:T(128)}, u32[]{:S(2)}) copy-start(s32[2]{0:T(128)} %param.12) | copy-start | bytes 28
  168.6 4.3 copy-start.3
  183.6 2.2 copy-start
  186.7 1.1 copy-start.6
  186.7 2.7 copy-start.4
  188.6 0.8 copy-start.7
  189.4 4.3 copy-start.3
  204.3 2.2 copy-start
  207.4 1.1 copy-start.6
  207.5 2.7 copy-start.4
  209.3 0.8 copy-start.7
Sparse Core Ops, SparseCore 0:
  10.7 74.2 all-gather.4
  87.8 74.1 all-gather.2
  223.0 355.6 reduce-scatter.1
where the time goes:
time: 639 us; the launch traced here: 638 us
  waiting for transfers between devices  486 us (76%)
  blocking collectives  49.1 us (8%)
  matrix products  39.9 us (6%)
  local copies, waits for them, and re-layouts  28.6 us (4%)
  other arithmetic  20 us (3%)
  between operations  14.5 us (2%)
    reduce_scatter x1, waiting for transfers between devices, local(): lax.psum_scatter(transposed_product(columns, combined), ('replica', 'fsdp...  356 us
    all_gather x1, waiting for transfers between devices, local(): lax.all_gather(key_master.astype(jnp.bfloat16), 'fsdp', axis=0, tiled=True)  71.2 us
    all_gather x1, waiting for transfers between devices, local(): lax.all_gather(value_master.astype(jnp.bfloat16), 'fsdp', axis=0, tiled=T...  58.6 us
    psum x1, blocking collectives, local(): total_sq = lax.psum(jnp.sum(owned_grad * owned_grad), ('replica', 'fsdp'))  44.4 us
    dynamic_slice x18, local copies, waits for them, and re-layouts, local(): lax.map(one_seq, (queries.reshape(seq_count, LEN, qwidth), key_proj.resha...  12.8 us
  transfers between devices with their start and end apart: 3, of which 3 were waited for; matrix products, arithmetic and copies ran while one was open for 3% of the time, Pallas kernels for 0%

commit v1 on v0

v1 whole, which is shorter than its diff:
```python
import functools

import jax
import jax.numpy as jnp
from jax import lax
from jax.experimental import pallas as pl
from jax.experimental.pallas import tpu as pltpu
from jax.sharding import PartitionSpec as P

HD = 128
LEN = 256
MESH = pl.DeviceIdType.MESH
F32 = jnp.float32
BF16 = jnp.bfloat16


def factor_chips(mesh):
    total = mesh.shape["fsdp"]
    axis = mesh.axis_names.index("fsdp")
    line = mesh.devices.swapaxes(0, axis).reshape(total, -1)[:, 0]
    coords = [tuple(getattr(d, "coords", ())) for d in line]
    extents = []
    step = total
    if all(len(c) == 3 for c in coords):
        while step > 1:
            found = None
            for axis3 in range(3):
                count = len({c[axis3] for c in coords[:step]})
                if count > 1 and step % count == 0:
                    inner = step // count
                    if all(len({coords[k * inner + i][axis3] for i in range(inner)}) == 1 for k in range(count)):
                        found = (count, inner)
            if found is None:
                break
            extents.append(found[0])
            step = found[1]
    if step > 1:
        extents = [total]
    while len(extents) < 3:
        extents.append(1)
    if len(extents) > 3:
        extents = [total, 1, 1]
    return tuple(extents)


class Place:
    def __init__(self, dims):
        self.n0, n1, n2 = dims
        self.core = lax.axis_index("replica")
        self.me = lax.axis_index("fsdp")
        self.plane = n1 * n2
        self.a = self.me // self.plane
        b = (self.me // n2) % n1
        c = self.me % n2
        self.b, self.c = b, c
        swap = self.core if n1 == n2 else 0
        self.nf, self.ns = n2, n1
        self.stride_f = 1 + swap * (n2 - 1)
        self.stride_s = n2 - swap * (n2 - 1)
        self.f = c + swap * (b - c)
        self.s = b + swap * (c - b)

    def block(self, ja, kf, ks):
        a = lax.rem(self.a + ja, self.n0)
        f = lax.rem(self.f + kf, self.nf)
        s = lax.rem(self.s + ks, self.ns)
        return a * self.plane + f * self.stride_f + s * self.stride_s


def loop(lower, upper, body):
    def step(i, carry):
        body(i)
        return carry

    if upper > lower:
        lax.fori_loop(lower, upper, step, 0)


def gather_kernel(
    dims, act_hbm, gain_ref, own_ref, kv_ref, xn_ref, act, weights, acc,
    act_sem, send_sem, recv_sem, pass_sem, peer_sem,
):
    at = Place(dims)
    n = weights.shape[1]
    half = at.core
    other = 1 - at.core
    tokens = act.shape[0]
    rows = own_ref.shape[1]
    fetch = pltpu.make_async_copy(act_hbm, act, act_sem)

    def to_chip(src, piece, dest, slot):
        return pltpu.make_async_remote_copy(
            src_ref=src, dst_ref=weights.at[half, piece], send_sem=send_sem.at[slot],
            recv_sem=recv_sem.at[piece], device_id={"replica": half, "fsdp": dest}, device_id_type=MESH,
        )

    def to_peer(piece):
        return pltpu.make_async_remote_copy(
            src_ref=weights.at[half, piece], dst_ref=weights.at[half, piece], send_sem=pass_sem.at[piece],
            recv_sem=peer_sem.at[piece], device_id={"replica": other, "fsdp": at.me}, device_id_type=MESH,
        )

    def from_peer(piece):
        return pltpu.make_async_remote_copy(
            src_ref=weights.at[other, piece], dst_ref=weights.at[other, piece], send_sem=pass_sem.at[piece],
            recv_sem=peer_sem.at[piece], device_id={"replica": other, "fsdp": at.me}, device_id_type=MESH,
        )

    base_f = at.n0 - 1
    base_s = base_f + at.n0 * (at.nf - 1)
    per_s = at.nf * (at.ns - 1)

    def forward_f(src, piece, j):
        loop(1, at.nf, lambda k: to_chip(
            src, piece, at.block(0, k, 0), base_f + j * (at.nf - 1) + k - 1).start())

    def forward_s(src, piece, j, kf):
        loop(1, at.ns, lambda k: to_chip(
            src, piece, at.block(0, 0, k), base_s + j * per_s + kf * (at.ns - 1) + k - 1).start())

    mine = own_ref.at[half]
    loop(1, at.n0, lambda j: to_chip(mine, at.me, at.block(j, 0, 0), j - 1).start())
    forward_f(mine, at.me, 0)
    forward_s(mine, at.me, 0, 0)
    fetch.start()
    acc[...] = jnp.zeros_like(acc)
    fetch.wait()

    chunk = 32

    def norm(i):
        part = act[pl.ds(pl.multiple_of(i * chunk, chunk), chunk), :].astype(F32)
        inverse = lax.rsqrt(jnp.mean(part * part, axis=-1, keepdims=True) + 1e-05)
        normed = (part * inverse * gain_ref[...]).astype(BF16)
        for p in range(n):
            xn_ref[p, pl.ds(pl.multiple_of(i * chunk, chunk), chunk), :] = normed[:, p * rows:(p + 1) * rows]

    loop(0, tokens // chunk, norm)

    def multiply(which, piece):
        acc[which] += jnp.dot(xn_ref[piece], weights[which, piece], preferred_element_type=F32)

    def arrive(piece, j, kf, kind):
        to_chip(mine, piece, at.me, 0).wait_recv()
        src = weights.at[half, piece]
        if kind == 0:
            forward_f(src, piece, j)
        if kind <= 1:
            forward_s(src, piece, j, kf)
        to_peer(piece).start()
        multiply(half, piece)

    for which in range(2):
        acc[which] += jnp.dot(xn_ref[at.me], own_ref[which], preferred_element_type=F32)
    for t in range(at.n0 + 2):
        if 1 <= t < at.n0:
            arrive(at.block(at.n0 - t, 0, 0), t, 0, 0)
        j = t - 1
        if 0 <= j < at.n0:
            loop(1, at.nf, lambda k: arrive(at.block(at.n0 - j, k, 0), j, k, 1))
        j2 = t - 2
        if 0 <= j2 < at.n0:
            loop(0, at.nf * (at.ns - 1), lambda k: arrive(
                at.block(at.n0 - j2, k // (at.ns - 1), k % (at.ns - 1) + 1), j2, 0, 2))

    def close(k):
        piece = lax.rem(at.me + k, n)
        from_peer(piece).wait_recv()
        multiply(other, piece)

    loop(1, n, close)
    loop(0, 2, lambda w: kv_ref.__setitem__(w, acc[w].astype(BF16)))
    loop(0, n - 1, lambda k: to_chip(mine, at.me, at.me, k).wait_send())
    loop(1, n, lambda k: to_peer(lax.rem(at.me + k, n)).wait_send())


def attend_kernel(group, lengths_ref, q_ref, g_ref, kv_ref, out_ref):
    seq = pl.program_id(0)
    length = lengths_ref[seq]
    scale = 1.0 / HD**0.5
    key_pos = lax.broadcasted_iota(jnp.int32, (LEN, LEN), 0)
    query_pos = lax.broadcasted_iota(jnp.int32, (LEN, LEN), 1)
    allowed = (key_pos <= query_pos) & (key_pos < length)
    live = lax.broadcasted_iota(jnp.int32, (LEN, HD), 0) < length
    key = kv_ref[0]
    value = kv_ref[1]
    last = (((1,), (1,)), ((), ()))
    key_grad = jnp.zeros((LEN, HD), F32)
    value_grad = jnp.zeros((LEN, HD), F32)
    for head in range(group):
        query = q_ref[:, head * HD:(head + 1) * HD]
        grad = jnp.where(live, g_ref[:, head * HD:(head + 1) * HD].astype(F32), 0.0)
        grad_low = grad.astype(BF16)
        grad_flip = grad.T
        scores = lax.dot_general(key, query, last, preferred_element_type=F32) * scale
        scores = jnp.where(allowed, scores, -1e30)
        peak = jnp.max(scores, axis=0, keepdims=True)
        exponent = jnp.exp(scores - peak)
        probs = exponent / jnp.sum(exponent, axis=0, keepdims=True)
        probs_low = probs.astype(BF16)
        attended = lax.dot_general(
            value, probs_low, (((0,), (0,)), ((), ())), preferred_element_type=F32).astype(BF16).astype(F32)
        delta = jnp.sum(grad_flip * attended, axis=0, keepdims=True)
        value_grad += jnp.dot(probs_low, grad_low, preferred_element_type=F32)
        prob_grad = lax.dot_general(value, grad_low, last, preferred_element_type=F32)
        score_grad = (probs * (prob_grad - delta)).astype(BF16)
        key_grad += jnp.dot(score_grad, query, preferred_element_type=F32)
    out_ref[0] = (key_grad * scale).astype(BF16)
    out_ref[1] = value_grad.astype(BF16)


def scatter_kernel(
    dims, count, xn_ref, dkv_ref, key_ref, value_ref, part, give, take, sendbuf, recvbuf, endbuf, sums,
    give_sem, take_sem, send_sem, recv_sem, end_send, end_recv, sum_send, sum_recv,
):
    at = Place(dims)
    n = part.shape[0]
    half = at.core
    other = 1 - at.core

    def to_peer(p):
        return pltpu.make_async_remote_copy(
            src_ref=give.at[p], dst_ref=take.at[p], send_sem=give_sem.at[p], recv_sem=take_sem.at[p],
            device_id={"replica": other, "fsdp": at.me}, device_id_type=MESH,
        )

    def to_chip(p, slot, dest):
        return pltpu.make_async_remote_copy(
            src_ref=sendbuf.at[p], dst_ref=recvbuf.at[slot], send_sem=send_sem.at[p],
            recv_sem=recv_sem.at[slot], device_id={"replica": half, "fsdp": dest}, device_id_type=MESH,
        )

    def compute(p):
        full = (((0,), (0,)), ((), ()))
        give[p] = lax.dot_general(
            xn_ref[p], dkv_ref[other], full, preferred_element_type=F32).astype(BF16)
        part[p] = lax.dot_general(xn_ref[p], dkv_ref[half], full, preferred_element_type=F32)
        to_peer(p).start()

    ahead = at.n0 * at.nf * (at.ns - 1)
    deep = ahead + at.n0 * (at.nf - 1)

    def slot_s(ja, kf, ks):
        a = lax.rem(at.a + ja, at.n0)
        f = lax.rem(at.f + kf, at.nf)
        return (ks - 1) * at.n0 * at.nf + a * at.nf + f

    def slot_f(ja, kf):
        return ahead + (kf - 1) * at.n0 + lax.rem(at.a + ja, at.n0)

    def slot_z(ja):
        return deep + ja - 1

    def landed(slot):
        to_chip(0, slot, at.me).wait_recv()
        return recvbuf[slot].astype(F32)

    def paired(p):
        to_peer(p).wait_recv()
        return part[p] + take[p].astype(F32)

    def gathered_s(ja, kf, p):
        total = paired(p)
        for ks in range(1, at.ns):
            total += landed(slot_s(ja, kf, ks))
        return total

    def gathered_f(ja, p):
        total = gathered_s(ja, 0, p)
        for kf in range(1, at.nf):
            total += landed(slot_f(ja, kf))
        return total

    def later(i):
        return lax.rem(i + 1, at.n0)

    def send_s(ja, kf, ks):
        p = at.block(ja, kf, ks)
        sendbuf[p] = paired(p).astype(BF16)
        to_chip(p, slot_s(ja, kf, ks), at.block(0, 0, ks)).start()

    def send_f(ja, kf):
        p = at.block(ja, kf, 0)
        sendbuf[p] = gathered_s(ja, kf, p).astype(BF16)
        to_chip(p, slot_f(ja, kf), at.block(0, kf, 0)).start()

    def send_z(ja):
        p = at.block(ja, 0, 0)
        sendbuf[p] = gathered_f(ja, p).astype(BF16)
        to_chip(p, slot_z(ja), p).start()

    ns1, nf1, n0 = at.ns - 1, at.nf - 1, at.n0
    loop(0, n0 * nf1 * ns1, lambda i: compute(
        at.block(later(i // (nf1 * ns1)), i // ns1 % nf1 + 1, i % ns1 + 1)))
    loop(0, n0 * nf1 * ns1, lambda i: send_s(
        later(i // (nf1 * ns1)), i // ns1 % nf1 + 1, i % ns1 + 1))
    loop(0, n0 * ns1, lambda i: compute(at.block(later(i // ns1), 0, i % ns1 + 1)))
    loop(0, n0 * nf1, lambda i: compute(at.block(later(i // nf1), i % nf1 + 1, 0)))
    loop(0, n0, lambda i: compute(at.block(i, 0, 0)))
    loop(0, n0 * ns1, lambda i: send_s(later(i // ns1), 0, i % ns1 + 1))
    loop(0, n0 * nf1, lambda i: send_f(later(i // nf1), i % nf1 + 1))
    loop(1, n0, send_z)
    owned = gathered_f(0, at.me)
    for ja in range(1, n0):
        owned += landed(slot_z(ja))
    endbuf[0] = owned.astype(BF16)

    trade = pltpu.make_async_remote_copy(
        src_ref=endbuf.at[0], dst_ref=endbuf.at[1], send_sem=end_send, recv_sem=end_recv,
        device_id={"replica": other, "fsdp": at.me}, device_id_type=MESH,
    )
    squares = jnp.sum(owned * owned)
    total = jnp.full((8, 128), squares, F32)
    n1, n2 = dims[1], dims[2]
    base = 0
    started = []
    for level, (size, digit, stride) in enumerate(
        ((n0, at.a, n1 * n2), (n1, at.b, n2), (n2, at.c, 1), (2, at.core, 0))
    ):
        if size > 1:
            sums[base + digit] = total
            for k in range(1, size):
                to = lax.rem(digit + k, size)
                if level == 3:
                    target = {"replica": other, "fsdp": at.me}
                else:
                    target = {"replica": half, "fsdp": at.me + (to - digit) * stride}
                copy = pltpu.make_async_remote_copy(
                    src_ref=sums.at[base + digit], dst_ref=sums.at[base + digit],
                    send_sem=sum_send.at[base + k], recv_sem=sum_recv.at[base + digit],
                    device_id=target, device_id_type=MESH,
                )
                copy.start()
                started.append(copy)
            if level == 0:
                trade.start()
            for k in range(1, size):
                came = lax.rem(digit + k, size)
                pltpu.make_async_remote_copy(
                    src_ref=sums.at[base + came], dst_ref=sums.at[base + came],
                    send_sem=sum_send.at[base + k], recv_sem=sum_recv.at[base + came],
                    device_id={"replica": other, "fsdp": at.me}, device_id_type=MESH,
                ).wait_recv()
            total = sums[base]
            for k in range(1, size):
                total += sums[base + k]
        elif level == 0:
            trade.start()
        base += size
    unit = jnp.sqrt(F32(count)) / jnp.sqrt(total + 1e-06)
    unit = unit[0:1, 0:1]
    trade.wait_recv()

    @pl.when(at.core == 0)
    def _():
        key_ref[...] = unit * endbuf[0].astype(F32)
        value_ref[...] = unit * endbuf[1].astype(F32)

    @pl.when(at.core == 1)
    def _():
        key_ref[...] = unit * endbuf[1].astype(F32)
        value_ref[...] = unit * endbuf[0].astype(F32)

    trade.wait_send()
    for copy in started:
        copy.wait_send()
    loop(0, n, lambda p: to_peer(p).wait_send())
    loop(1, n, lambda k: to_chip(lax.rem(at.me + k, n), 0, at.me).wait_send())


VMEM = pl.BlockSpec(memory_space=pltpu.VMEM)
LIMIT = 60 * 1024 * 1024


def local(dims, activations, queries, out_grad, lengths, norm_gain, key_master, value_master):
    tokens, features = activations.shape
    rows, width = key_master.shape
    n = features // rows
    qwidth = queries.shape[1]
    group = qwidth // width
    heads = width // HD
    seqs = lengths.shape[0]
    own = jnp.stack([key_master.astype(BF16), value_master.astype(BF16)])
    dma = pltpu.SemaphoreType.DMA
    kv, xn = pl.pallas_call(
        functools.partial(gather_kernel, dims),
        out_shape=(
            jax.ShapeDtypeStruct((2, tokens, width), BF16),
            jax.ShapeDtypeStruct((n, tokens, rows), BF16),
        ),
        in_specs=[pl.BlockSpec(memory_space=pl.ANY), VMEM, VMEM],
        out_specs=(VMEM, VMEM),
        scratch_shapes=[
            pltpu.VMEM((tokens, features), BF16),
            pltpu.VMEM((2, n, rows, width), BF16),
            pltpu.VMEM((2, tokens, width), F32),
            dma, dma((n,)), dma((n,)), dma((n,)), dma((n,)),
        ],
        compiler_params=pltpu.CompilerParams(has_side_effects=True, vmem_limit_bytes=LIMIT),
    )(activations, norm_gain.reshape(1, features), own)
    dkv = pl.pallas_call(
        functools.partial(attend_kernel, group),
        out_shape=jax.ShapeDtypeStruct((2, tokens, width), BF16),
        grid=(seqs, heads),
        in_specs=[
            pl.BlockSpec(memory_space=pltpu.SMEM),
            pl.BlockSpec((LEN, group * HD), lambda s, h: (s, h)),
            pl.BlockSpec((LEN, group * HD), lambda s, h: (s, h)),
            pl.BlockSpec((2, LEN, HD), lambda s, h: (0, s, h)),
        ],
        out_specs=pl.BlockSpec((2, LEN, HD), lambda s, h: (0, s, h)),
    )(lengths, queries, out_grad, kv)
    shape = jax.ShapeDtypeStruct((rows, width), F32)
    return pl.pallas_call(
        functools.partial(scatter_kernel, dims, 2 * features * width),
        out_shape=(shape, shape),
        in_specs=[VMEM, VMEM],
        out_specs=(VMEM, VMEM),
        scratch_shapes=[
            pltpu.VMEM((n, rows, width), F32),
            pltpu.VMEM((n, rows, width), BF16),
            pltpu.VMEM((n, rows, width), BF16),
            pltpu.VMEM((n, rows, width), BF16),
            pltpu.VMEM((n, rows, width), BF16),
            pltpu.VMEM((2, rows, width), BF16),
            pltpu.VMEM((sum(dims) + 2, 8, 128), F32),
            dma((n,)), dma((n,)), dma((n,)), dma((n,)), dma, dma,
            dma((sum(dims) + 2,)), dma((sum(dims) + 2,)),
        ],
        compiler_params=pltpu.CompilerParams(has_side_effects=True, vmem_limit_bytes=LIMIT),
    )(xn, dkv)


def solution(mesh):
    in_specs = (
        P(("replica", "fsdp"), None),
        P(("replica", "fsdp"), None),
        P(("replica", "fsdp"), None),
        P(("replica", "fsdp")),
        P(),
        P("fsdp", None),
        P("fsdp", None),
    )
    out_specs = (P("fsdp", None), P("fsdp", None))
    body = functools.partial(local, factor_chips(mesh))
    return jax.shard_map(body, mesh=mesh, in_specs=in_specs, out_specs=out_specs, check_vma=False)
```

time: 639 us -> 155 us (0.24)
  waiting for transfers between devices: 486 us -> 0 us
  Pallas kernels: 0 us -> 147 us
  blocking collectives: 49.1 us -> 0 us
  matrix products: 39.9 us -> 0 us
  local copies, waits for them, and re-layouts: 28.6 us -> 3.74 us
  other arithmetic: 20 us -> 2.11 us
  between operations: 14.5 us -> 0.65 us
    reduce_scatter x1 -> x0, waiting for transfers between devices: 356 us -> none  [local(): lax.psum_scatter(transposed_product(columns, combined), ('replica', 'fsdp...]
    pallas_call x0 -> x3, Pallas kernels: none -> 147 us  [the longest x1 73.4 us: local(): pl.pallas_call(functools.partial(scatter_kernel, dims, 2 * features * wid...]
    all_gather x2 -> x0, waiting for transfers between devices: 130 us -> none  [the longest x1 71.2 us: local(): lax.all_gather(key_master.astype(jnp.bfloat16), 'fsdp', axis=0, tiled=True)]
    psum x1 -> x0, blocking collectives: 44.4 us -> none  [local(): total_sq = lax.psum(jnp.sum(owned_grad * owned_grad), ('replica', 'fsdp'))]
    dot_general x11 -> x0, matrix products: 31.1 us -> none  [the longest x1 12.7 us: transposed_product(): lax.dot_general(columns, combined, (((0,), (0,)), ((), ())), preferred_el...]
    dynamic_slice x18 -> x0, local copies, waits for them, and re-layouts: 12.8 us -> none  [local(): lax.map(one_seq, (queries.reshape(seq_count, LEN, qwidth), key_proj.resha...]
    convert_element_type x8 -> x0, other arithmetic: 11.3 us -> none  [the longest x2 5.23 us: attend(): probs_low = lax.optimization_barrier(probs.astype(jnp.bfloat16))]
    sub x2 -> x0, matrix products: 8.81 us -> none  [attend(): exponent = jnp.exp(scores - row_peak)]
  transfers between devices with their start and end apart: 3 -> 0, of which waited for: 3 -> 0; matrix products, arithmetic and copies ran while one was open for 3% -> 0% of each run, Pallas kernels for 0% -> 0%
where the time goes in v1:
time: 155 us; the launch traced here: 153 us
  Pallas kernels  147 us (95%)
  local copies, waits for them, and re-layouts  3.74 us (2%)
  other arithmetic  2.11 us (1%)
    pallas_call x1, Pallas kernels, local(): pl.pallas_call(functools.partial(scatter_kernel, dims, 2 * features * wid...  73.4 us
    pallas_call x1, Pallas kernels, local(): pl.pallas_call(functools.partial(gather_kernel, dims), out_shape=(jax.Sha...  57.3 us
    pallas_call x1, Pallas kernels, local(): pl.pallas_call(functools.partial(attend_kernel, group), out_shape=jax.Sha...  15.9 us
    unnamed x2, local copies, waits for them, and re-layouts  3.74 us

profile of v1, /device:TPU:7, one launch (start us, length us, event | category | flops | bytes accessed | tf_op | source)
XLA Modules:
  0.0 153.1 jit_solution(16199232101481795465)
XLA Ops:
  0.6 1.3 convert_bitcast_fusion
  1.9 0.8 pad_maximum_fusion.own_ref
  2.7 57.3 %shard_map.86 = (bf16[2,512,512]{2,1,0:T(8,128)(2,1)}, bf16[16,512,256]{2,1,0:T(8,128)(2,1)}) custom-call(bf16[512,4096]{1,0:T(8,128)(2,1)} %act_hbm.1, f32[1,4096]{1,0:T(1,128)} %bitcast.5, bf16[2,256,512]{2,1,0:T(8,128)(2,1)} %pad_maximum_fusion.own_ref), custom_call_target="tpu_custom_call" | custom-call | tf_op jit(solution)/shard_map/pallas_call | solution.py:385
  60.0 15.9 %shard_map.87.dkv_ref = bf16[2,512,512]{2,1,0:T(8,128)(2,1)} custom-call(s32[2]{0:T(128)} %lengths_ref.1, bf16[512,2048]{1,0:T(8,128)(2,1)} %q_ref.1, bf16[512,2048]{1,0:T(8,128)(2,1)} %g_ref.1, bf16[2,512,512]{2,1,0:T(8,128)(2,1)} %get-tuple-element.5.kv_ref), custom_call_target="tpu_custom_call" | custom-call | tf_op jit(solution)/shard_map/pallas_call | solution.py:401
  75.9 73.4 %shard_map.88 = (f32[256,512]{1,0:T(8,128)}, f32[256,512]{1,0:T(8,128)}) custom-call(bf16[16,512,256]{2,1,0:T(8,128)(2,1)} %get-tuple-element.4.xn_ref, bf16[2,512,512]{2,1,0:T(8,128)(2,1)} %shard_map.87.dkv_ref), custom_call_target="tpu_custom_call" | custom-call | tf_op jit(solution)/shard_map/pallas_call | solution.py:414
  149.4 1.9 %copy.11 = f32[256,512]{1,0:T(8,128)} copy(f32[256,512]{1,0:T(8,128)} %get-tuple-element.10) | data formatting | bytes 1048576
  151.2 1.9 %copy.12 = f32[256,512]{1,0:T(8,128)} copy(f32[256,512]{1,0:T(8,128)} %get-tuple-element.11) | data formatting | bytes 1048576

commit v2 on v1

--- a/solution.py
+++ b/solution.py
@@ -78,7 +78,7 @@
 
 def gather_kernel(
     dims, act_hbm, gain_ref, own_ref, kv_ref, xn_ref, act, weights, acc,
-    act_sem, send_sem, recv_sem, pass_sem, peer_sem,
+    act_sem, send_sem, recv_sem, pass_sem, peer_sem, line_sem,
 ):
     at = Place(dims)
     n = weights.shape[1]
@@ -106,7 +106,15 @@
             recv_sem=peer_sem.at[piece], device_id={"replica": other, "fsdp": at.me}, device_id_type=MESH,
         )
 
-    base_f = at.n0 - 1
+    def along(src, piece, a, slot):
+        dest = at.me + (a - at.a) * at.plane
+        return pltpu.make_async_remote_copy(
+            src_ref=src, dst_ref=weights.at[half, piece], send_sem=line_sem.at[slot],
+            recv_sem=recv_sem.at[piece], device_id={"replica": half, "fsdp": dest}, device_id_type=MESH,
+        )
+
+    n0, a = at.n0, at.a
+    base_f = 0
     base_s = base_f + at.n0 * (at.nf - 1)
     per_s = at.nf * (at.ns - 1)
 
@@ -119,7 +127,8 @@
             src, piece, at.block(0, 0, k), base_s + j * per_s + kf * (at.ns - 1) + k - 1).start())
 
     mine = own_ref.at[half]
-    loop(1, at.n0, lambda j: to_chip(mine, at.me, at.block(j, 0, 0), j - 1).start())
+    pl.when(a + 1 < n0)(lambda: along(mine, at.me, a + 1, n0).start())
+    pl.when(a > 0)(lambda: along(mine, at.me, a - 1, n0 + 1).start())
     forward_f(mine, at.me, 0)
     forward_s(mine, at.me, 0, 0)
     fetch.start()
@@ -140,28 +149,45 @@
     def multiply(which, piece):
         acc[which] += jnp.dot(xn_ref[piece], weights[which, piece], preferred_element_type=F32)
 
-    def arrive(piece, j, kf, kind):
+    def arrive(piece, j, kf):
         to_chip(mine, piece, at.me, 0).wait_recv()
-        src = weights.at[half, piece]
-        if kind == 0:
-            forward_f(src, piece, j)
-        if kind <= 1:
-            forward_s(src, piece, j, kf)
+        if kf is not None:
+            forward_s(weights.at[half, piece], piece, j, kf)
         to_peer(piece).start()
         multiply(half, piece)
 
     for which in range(2):
         acc[which] += jnp.dot(xn_ref[at.me], own_ref[which], preferred_element_type=F32)
-    for t in range(at.n0 + 2):
-        if 1 <= t < at.n0:
-            arrive(at.block(at.n0 - t, 0, 0), t, 0, 0)
-        j = t - 1
-        if 0 <= j < at.n0:
-            loop(1, at.nf, lambda k: arrive(at.block(at.n0 - j, k, 0), j, k, 1))
-        j2 = t - 2
-        if 0 <= j2 < at.n0:
-            loop(0, at.nf * (at.ns - 1), lambda k: arrive(
-                at.block(at.n0 - j2, k // (at.ns - 1), k % (at.ns - 1) + 1), j2, 0, 2))
+    def first(step, away):
+        piece = at.me + step * away * at.plane
+        to_chip(mine, piece, at.me, 0).wait_recv()
+        nearer = a - step
+        pl.when((nearer >= 0) & (nearer < n0))(
+            lambda: along(weights.at[half, piece], piece, nearer, a + step * away).start())
+        src = weights.at[half, piece]
+        j = lax.rem(n0 + step * away, n0)
+        forward_f(src, piece, j)
+        forward_s(src, piece, j, 0)
+        to_peer(piece).start()
+        multiply(half, piece)
+
+    def second(step, away):
+        j = lax.rem(n0 + step * away, n0)
+        loop(1, at.nf, lambda k: arrive(at.block(j, k, 0), j, k))
+
+    def third(step, away):
+        j = lax.rem(n0 + step * away, n0)
+        loop(0, at.nf * (at.ns - 1), lambda k: arrive(
+            at.block(j, k // (at.ns - 1), k % (at.ns - 1) + 1), j, None))
+
+    for t in range(n0 + 2):
+        for lag, work in enumerate((first, second, third)):
+            away = t - lag
+            if away == 0 and lag > 0:
+                work(1, 0)
+            elif 0 < away < n0:
+                pl.when(a - away >= 0)(lambda: work(-1, away))
+                pl.when(a + away < n0)(lambda: work(1, away))
 
     def close(k):
         piece = lax.rem(at.me + k, n)
@@ -170,7 +196,12 @@
 
     loop(1, n, close)
     loop(0, 2, lambda w: kv_ref.__setitem__(w, acc[w].astype(BF16)))
-    loop(0, n - 1, lambda k: to_chip(mine, at.me, at.me, k).wait_send())
+    loop(0, n - n0, lambda k: to_chip(mine, at.me, at.me, k).wait_send())
+    pl.when(a + 1 < n0)(lambda: along(mine, at.me, a, n0).wait_send())
+    pl.when(a > 0)(lambda: along(mine, at.me, a, n0 + 1).wait_send())
+    for k in range(n0):
+        pl.when(((k < a) & (a + 1 < n0)) | ((k > a) & (a > 0)))(
+            lambda: along(mine, at.me, a, k).wait_send())
     loop(1, n, lambda k: to_peer(lax.rem(at.me + k, n)).wait_send())
 
 
@@ -210,7 +241,7 @@
 
 
 def scatter_kernel(
-    dims, count, xn_ref, dkv_ref, key_ref, value_ref, part, give, take, sendbuf, recvbuf, endbuf, sums,
+    dims, count, xn_ref, dkv_ref, both_ref, unit_ref, part, give, take, sendbuf, recvbuf, endbuf, sums,
     give_sem, take_sem, send_sem, recv_sem, end_send, end_recv, sum_send, sum_recv,
 ):
     at = Place(dims)
@@ -348,19 +379,10 @@
             trade.start()
         base += size
     unit = jnp.sqrt(F32(count)) / jnp.sqrt(total + 1e-06)
-    unit = unit[0:1, 0:1]
+    unit_ref[...] = unit
+    both_ref[half] = endbuf[0]
     trade.wait_recv()
-
-    @pl.when(at.core == 0)
-    def _():
-        key_ref[...] = unit * endbuf[0].astype(F32)
-        value_ref[...] = unit * endbuf[1].astype(F32)
-
-    @pl.when(at.core == 1)
-    def _():
-        key_ref[...] = unit * endbuf[1].astype(F32)
-        value_ref[...] = unit * endbuf[0].astype(F32)
-
+    both_ref[other] = endbuf[1]
     trade.wait_send()
     for copy in started:
         copy.wait_send()
@@ -394,7 +416,7 @@
             pltpu.VMEM((tokens, features), BF16),
             pltpu.VMEM((2, n, rows, width), BF16),
             pltpu.VMEM((2, tokens, width), F32),
-            dma, dma((n,)), dma((n,)), dma((n,)), dma((n,)),
+            dma, dma((n,)), dma((n,)), dma((n,)), dma((n,)), dma((dims[0] + 2,)),
         ],
         compiler_params=pltpu.CompilerParams(has_side_effects=True, vmem_limit_bytes=LIMIT),
     )(activations, norm_gain.reshape(1, features), own)
@@ -410,10 +432,9 @@
         ],
         out_specs=pl.BlockSpec((2, LEN, HD), lambda s, h: (0, s, h)),
     )(lengths, queries, out_grad, kv)
-    shape = jax.ShapeDtypeStruct((rows, width), F32)
-    return pl.pallas_call(
+    both, unit = pl.pallas_call(
         functools.partial(scatter_kernel, dims, 2 * features * width),
-        out_shape=(shape, shape),
+        out_shape=(jax.ShapeDtypeStruct((2, rows, width), BF16), jax.ShapeDtypeStruct((8, 128), F32)),
         in_specs=[VMEM, VMEM],
         out_specs=(VMEM, VMEM),
         scratch_shapes=[
@@ -429,6 +450,8 @@
         ],
         compiler_params=pltpu.CompilerParams(has_side_effects=True, vmem_limit_bytes=LIMIT),
     )(xn, dkv)
+    scale = unit[0, 0]
+    return scale * both[0].astype(F32), scale * both[1].astype(F32)
 
 
 def solution(mesh):

time: 155 us -> 147 us (0.948)
  Pallas kernels: 147 us -> 138 us
  other arithmetic: 2.11 us -> 4.85 us
  local copies, waits for them, and re-layouts: 3.74 us -> 1.22 us
    pallas_call x1, Pallas kernels: 57.3 us -> 52.4 us  [local(): pl.pallas_call(functools.partial(gather_kernel, dims), out_shape=(jax.Sha...]
    pallas_call x1, Pallas kernels: 73.4 us -> 69.6 us  [local(): pl.pallas_call(functools.partial(scatter_kernel, dims, 2 * features * wid...]
    unnamed x2 -> x0, local copies, waits for them, and re-layouts: 3.74 us -> none
    mul x0 -> x1, other arithmetic: none -> 2.75 us  [local(): return (scale * both[0].astype(F32), scale * both[1].astype(F32))]
where the time goes in v2:
time: 147 us; the launch traced here: 145 us
  Pallas kernels  138 us (94%)
  other arithmetic  4.85 us (3%)
    pallas_call x1, Pallas kernels, local(): pl.pallas_call(functools.partial(scatter_kernel, dims, 2 * features * wid...  69.6 us
    pallas_call x1, Pallas kernels, local(): pl.pallas_call(functools.partial(gather_kernel, dims), out_shape=(jax.Sha...  52.4 us
    pallas_call x1, Pallas kernels, local(): pl.pallas_call(functools.partial(attend_kernel, group), out_shape=jax.Sha...  15.9 us

profile of v2, /device:TPU:7, one launch (start us, length us, event | category | flops | bytes accessed | tf_op | source)
XLA Modules:
  0.0 144.7 jit_solution(5464341131195050269)
XLA Ops:
  0.6 1.3 convert_bitcast_fusion
  1.9 0.8 pad_maximum_fusion.own_ref
  2.7 52.4 %shard_map.86 = (bf16[2,512,512]{2,1,0:T(8,128)(2,1)}, bf16[16,512,256]{2,1,0:T(8,128)(2,1)}) custom-call(bf16[512,4096]{1,0:T(8,128)(2,1)} %act_hbm.1, f32[1,4096]{1,0:T(1,128)} %bitcast.10, bf16[2,256,512]{2,1,0:T(8,128)(2,1)} %pad_maximum_fusion.own_ref), custom_call_target="tpu_custom_call" | custom-call | tf_op jit(solution)/shard_map/pallas_call | solution.py:407
  55.2 15.9 %shard_map.87.dkv_ref = bf16[2,512,512]{2,1,0:T(8,128)(2,1)} custom-call(s32[2]{0:T(128)} %lengths_ref.1, bf16[512,2048]{1,0:T(8,128)(2,1)} %q_ref.1, bf16[512,2048]{1,0:T(8,128)(2,1)} %g_ref.1, bf16[2,512,512]{2,1,0:T(8,128)(2,1)} %get-tuple-element.7.kv_ref), custom_call_target="tpu_custom_call" | custom-call | tf_op jit(solution)/shard_map/pallas_call | solution.py:423
  71.1 69.6 %shard_map.88 = (bf16[2,256,512]{2,1,0:T(8,128)(2,1)}, f32[8,128]{1,0:T(8,128)}) custom-call(bf16[16,512,256]{2,1,0:T(8,128)(2,1)} %get-tuple-element.6.xn_ref, bf16[2,512,512]{2,1,0:T(8,128)(2,1)} %shard_map.87.dkv_ref), custom_call_target="tpu_custom_call" | custom-call | tf_op jit(solution)/shard_map/pallas_call | solution.py:435
  140.7 1.2 slice.9
  141.9 2.7 %multiply_bitcast_fusion = (f32[256,512]{1,0:T(8,128)}, f32[256,512]{1,0:T(8,128)}) fusion(bf16[2,256,512]{2,1,0:T(8,128)(2,1)} %get-tuple-element.9, f32[]{:T(128)} %bitcast.3), kind=kLoop, calls=%fused_computation.1 | loop fusion | flops 524288 | bytes 1572868 | tf_op jit(solution)/shard_map/mul | solution.py:454
